TPU v7x, 32 devices: a whole 2x2x4 slice. The times are simulated.
32 devices in a mesh: batch: 4 (over z), row: 4 (over x, core), col: 2 (over y).
Axes of the slice: x: 2, y: 2, z: 4, core: 2. Of those that a mesh axis runs over, the one named last changes fastest.
Arguments:
- flows: float32 [32768, 8192], P(('batch', 'row'), 'col'), parts along dimension 0, may hold values from 0 to 21, as said below
- tile_mask: int32 [256, 64], P(('batch', 'row'), 'col'), parts along dimension 0, may hold values from 0 to 1, as said below
- row_target: int32 [32768], P(('batch', 'row')), parts along dimension 0, may hold values from 1638400 to 8191999
- col_target: int32 [32768], P(('batch', 'col')), parts along dimension 0, may hold values from 1638400 to 8191999
Outputs:
- row_history: float32 [12, 8192], P('batch', 'row'), parts along dimension 0
- col_history: float32 [12, 8192], P('batch', 'col'), parts along dimension 0
There are 4 independent parts, one for each index of `batch`. A program takes and returns all parts, laid end to end along the dimension named above; each array names one. Nothing has to cross between parts.
Inputs may be any that keep to these rules, and one draw needn't show every extreme that they name: `tile_mask`: every diagonal tile is 1. `flows`: every entry is positive.
All inputs are finite; a program needn't handle non-finite values.
Results may differ from a plain program's by a relative error of at most 0.0001.
Values sent between devices are 32-bit elements; how exact they have to be, the bound alone decides.
A program may use at most 192 MiB of HBM per device.

v0:
```python
import jax
import jax.numpy as jnp
from jax import lax
from jax.sharding import PartitionSpec as P

ITERS = 3


def block_sweeps(active, row_goal, col_goal):
    row_count, col_count = active.shape
    row_hist = jnp.zeros((ITERS, row_count), jnp.float32)
    col_hist = jnp.zeros((ITERS, col_count), jnp.float32)
    col_scale = jnp.ones((col_count,), jnp.float32)

    def advance(sweep_index, carry):
        col_scale, row_hist, col_hist = carry
        row_part = jnp.sum(active * col_scale[None, :], axis=1)
        row_total = lax.psum(row_part, "col")
        row_scale = row_goal / row_total
        col_part = jnp.sum(active * row_scale[:, None], axis=0)
        col_total = lax.psum(col_part, "row")
        col_scale = col_goal / col_total
        row_hist = lax.dynamic_update_slice_in_dim(row_hist, row_scale[None, :], sweep_index, 0)
        col_hist = lax.dynamic_update_slice_in_dim(col_hist, col_scale[None, :], sweep_index, 0)
        return (col_scale, row_hist, col_hist)

    col_scale, row_hist, col_hist = lax.fori_loop(
        0, ITERS, advance, (col_scale, row_hist, col_hist)
    )
    return (row_hist, col_hist)


def shards(flows, tile_mask, row_target, col_target):
    row_count, col_count = flows.shape
    tile_side = row_count // tile_mask.shape[0]
    expand = tile_mask.astype(jnp.float32)[:, None, :, None]
    active = (
        flows.reshape(row_count // tile_side, tile_side, col_count // tile_side, tile_side) * expand
    ).reshape(row_count, col_count)
    row_goal = row_target.astype(jnp.float32) * 0.001
    col_goal = col_target.astype(jnp.float32) * 0.001
    row_hist, col_hist = block_sweeps(active, row_goal, col_goal)
    return (row_hist, col_hist)


def solution(mesh):
    return jax.shard_map(
        shards,
        mesh=mesh,
        in_specs=(
            P(("batch", "row"), "col"),
            P(("batch", "row"), "col"),
            P(("batch", "row")),
            P(("batch", "col")),
        ),
        out_specs=(P("batch", "row"), P("batch", "col")),
        check_vma=False,
    )
```

profile of v0, /device:TPU:0, one launch (start us, length us, event | category | flops | bytes accessed | tf_op | source)
XLA Modules:
  0.0 185.6 jit_solution(14115084264689669346)
XLA Ops:
  0.6 0.7 convert_element_type.9
  1.3 11.2 %mul.63 = f32[16,128,32,128]{3,2,1,0:T(8,128)} broadcast(f32[16,32]{1,0:T(8,128)S(1)} %convert_element_type.9), dimensions={0,2} | broadcast | bytes 33556480 | tf_op jit(solution)/shard_map/mul | solution.py:38
  12.6 0.0 copy-start
  12.6 0.0 copy-start.1
  12.6 42.4 %bitcast_multiply_fusion = f32[2048,4096]{1,0:T(8,128)} fusion(f32[2048,4096]{1,0:T(8,128)} %param.6, f32[256,8,32,128]{3,2,1,0:T(8,128)} %bitcast.10), kind=kLoop, calls=%fused_computation.3 | loop fusion | flops 8388608 | bytes 100663296 | tf_op jit(solution)/shard_map/mul | solution.py:38
  55.0 0.0 copy-done
  55.0 0.0 copy-done.1
  55.0 130.6 %while.18 = (s32[]{:T(128)}, f32[4096]{0:T(1024)S(1)}, f32[3,2048]{1,0:T(4,128)}, f32[3,4096]{1,0:T(4,128)}, f32[2048,4096]{1,0:T(8,128)}, /*index=5*/f32[2048]{0:T(1024)S(1)}, f32[4096]{0:T(1024)S(1)}, s32[]{:T(128)}, s32[]{:T(128)}) while((s32[]{:T(128)}, f32[4096]{0:T(1024)S(1)}, f32[3,2048]{1,0:T(4,128)}, f32[3,4096]{1,0:T(4,128)}, ...), condition=%wide.region_5.0_spmd.clone, body=%wide.region_0.0_spmd.clone.sunk | while | flops 33564672 | bytes 67362928 | solution.py:27
  55.1 12.3 %multiply_reduce_fusion.4 = f32[2048]{0:T(1024)S(1)} fusion(f32[2048,4096]{1,0:T(8,128)} %get-tuple-element.232, f32[4096]{0:T(1024)S(1)} %broadcast_select_fusion.2), kind=kLoop, calls=%fused_computation.1.clone.1 | loop fusion | flops 16775168 | bytes 33579008 | tf_op jit(solution)/shard_map/while/body/eval_jaxpr/reduce_sum | solution.py:17
  67.3 6.0 %psum.26 = f32[2048]{0:T(1024)S(1)} all-reduce(f32[2048]{0:T(1024)S(1)} %multiply_reduce_fusion.4), channel_id=1, replica_groups=mesh['batch'=4,'row'=4,'col'=2] {'col'}, use_global_device_ids=true, to_apply=%region_2.0 | all-reduce | flops 2048 | bytes 16384 | tf_op jit(solution)/shard_map/while/body/eval_jaxpr/psum | solution.py:18
  73.3 12.8 %multiply_reduce_fusion.5 = f32[4096]{0:T(1024)S(1)} fusion(f32[2048,4096]{1,0:T(8,128)} %get-tuple-element.232, f32[2048]{0:T(1024)S(1)} %div.18), kind=kLoop, calls=%fused_computation.clone.1 | loop fusion | flops 16773120 | bytes 33579008 | tf_op jit(solution)/shard_map/while/body/eval_jaxpr/reduce_sum | solution.py:20
  86.1 10.3 %psum.27 = f32[4096]{0:T(1024)S(1)} all-reduce(f32[4096]{0:T(1024)S(1)} %multiply_reduce_fusion.5), channel_id=1, replica_groups=mesh['batch'=4,'row'=4,'col'=2] {'row'}, use_global_device_ids=true, to_apply=%region_4.0 | all-reduce | flops 4096 | bytes 32768 | tf_op jit(solution)/shard_map/while/body/eval_jaxpr/psum | solution.py:21
  96.4 1.5 dynamic_update_slice.19
  97.9 1.4 dynamic_update_slice.18
  99.3 12.2 %multiply_reduce_fusion.4 = f32[2048]{0:T(1024)S(1)} fusion(f32[2048,4096]{1,0:T(8,128)} %get-tuple-element.232, f32[4096]{0:T(1024)S(1)} %broadcast_select_fusion.2), kind=kLoop, calls=%fused_computation.1.clone.1 | loop fusion | flops 16775168 | bytes 33579008 | tf_op jit(solution)/shard_map/while/body/eval_jaxpr/reduce_sum | solution.py:17
  111.6 5.0 %psum.26 = f32[2048]{0:T(1024)S(1)} all-reduce(f32[2048]{0:T(1024)S(1)} %multiply_reduce_fusion.4), channel_id=1, replica_groups=mesh['batch'=4,'row'=4,'col'=2] {'col'}, use_global_device_ids=true, to_apply=%region_2.0 | all-reduce | flops 2048 | bytes 16384 | tf_op jit(solution)/shard_map/while/body/eval_jaxpr/psum | solution.py:18
  116.6 12.8 %multiply_reduce_fusion.5 = f32[4096]{0:T(1024)S(1)} fusion(f32[2048,4096]{1,0:T(8,128)} %get-tuple-element.232, f32[2048]{0:T(1024)S(1)} %div.18), kind=kLoop, calls=%fused_computation.clone.1 | loop fusion | flops 16773120 | bytes 33579008 | tf_op jit(solution)/shard_map/while/body/eval_jaxpr/reduce_sum | solution.py:20
  129.4 10.1 %psum.27 = f32[4096]{0:T(1024)S(1)} all-reduce(f32[4096]{0:T(1024)S(1)} %multiply_reduce_fusion.5), channel_id=1, replica_groups=mesh['batch'=4,'row'=4,'col'=2] {'row'}, use_global_device_ids=true, to_apply=%region_4.0 | all-reduce | flops 4096 | bytes 32768 | tf_op jit(solution)/shard_map/while/body/eval_jaxpr/psum | solution.py:21
  139.5 1.5 dynamic_update_slice.19
  141.1 1.4 dynamic_update_slice.18
  142.5 12.2 %multiply_reduce_fusion.4 = f32[2048]{0:T(1024)S(1)} fusion(f32[2048,4096]{1,0:T(8,128)} %get-tuple-element.232, f32[4096]{0:T(1024)S(1)} %broadcast_select_fusion.2), kind=kLoop, calls=%fused_computation.1.clone.1 | loop fusion | flops 16775168 | bytes 33579008 | tf_op jit(solution)/shard_map/while/body/eval_jaxpr/reduce_sum | solution.py:17
  154.7 5.0 %psum.26 = f32[2048]{0:T(1024)S(1)} all-reduce(f32[2048]{0:T(1024)S(1)} %multiply_reduce_fusion.4), channel_id=1, replica_groups=mesh['batch'=4,'row'=4,'col'=2] {'col'}, use_global_device_ids=true, to_apply=%region_2.0 | all-reduce | flops 2048 | bytes 16384 | tf_op jit(solution)/shard_map/while/body/eval_jaxpr/psum | solution.py:18
  159.7 12.8 %multiply_reduce_fusion.5 = f32[4096]{0:T(1024)S(1)} fusion(f32[2048,4096]{1,0:T(8,128)} %get-tuple-element.232, f32[2048]{0:T(1024)S(1)} %div.18), kind=kLoop, calls=%fused_computation.clone.1 | loop fusion | flops 16773120 | bytes 33579008 | tf_op jit(solution)/shard_map/while/body/eval_jaxpr/reduce_sum | solution.py:20
  172.5 10.1 %psum.27 = f32[4096]{0:T(1024)S(1)} all-reduce(f32[4096]{0:T(1024)S(1)} %multiply_reduce_fusion.5), channel_id=1, replica_groups=mesh['batch'=4,'row'=4,'col'=2] {'row'}, use_global_device_ids=true, to_apply=%region_4.0 | all-reduce | flops 4096 | bytes 32768 | tf_op jit(solution)/shard_map/while/body/eval_jaxpr/psum | solution.py:21
  182.7 1.5 dynamic_update_slice.19
  184.2 1.4 dynamic_update_slice.18
  (14 shorter events, 0.1 us)
Async XLA Ops:
  12.6 42.4 %copy-start = (s32[4096]{0:T(1024)S(1)}, s32[4096]{0:T(1024)}, u32[]{:S(2)}) copy-start(s32[4096]{0:T(1024)} %param.9) | copy-start | bytes 49156
  12.6 42.5 %copy-start.1 = (s32[2048]{0:T(1024)S(1)}, s32[2048]{0:T(1024)}, u32[]{:S(2)}) copy-start(s32[2048]{0:T(1024)} %param.8) | copy-start | bytes 24580
where the time goes:
time: 187 us; the launch traced here: 186 us
  other arithmetic  118 us (63%)
  blocking collectives  46.5 us (25%)
  local copies, waits for them, and re-layouts  20.1 us (11%)
    mul x1, other arithmetic, shards(): flows.reshape(row_count // tile_side, tile_side, col_count // tile_side,...  42.4 us
    reduce_sum x3, other arithmetic, advance(): col_part = jnp.sum(active * row_scale[:, None], axis=0)  38.4 us
    reduce_sum x3, other arithmetic, advance(): row_part = jnp.sum(active * col_scale[None, :], axis=1)  36.8 us
    psum x3, blocking collectives, advance(): col_total = lax.psum(col_part, 'row')  30.5 us
    psum x3, blocking collectives, advance(): row_total = lax.psum(row_part, 'col')  16 us
    mul x1, local copies, waits for them, and re-layouts, shards(): flows.reshape(row_count // tile_side, tile_side, col_count // tile_side,...  11.2 us
    dynamic_update_slice x3, local copies, waits for them, and re-layouts, advance(): lax.dynamic_update_slice_in_dim(col_hist, col_scale[None, :], sweep_index...  4.64 us
    dynamic_update_slice x3, local copies, waits for them, and re-layouts, advance(): lax.dynamic_update_slice_in_dim(row_hist, row_scale[None, :], sweep_index...  4.23 us

commit v1 on v0

v1 whole, which is shorter than its diff:
```python
import functools

import jax
import jax.numpy as jnp
from jax import lax
from jax.experimental import pallas as pl
from jax.experimental.pallas import tpu as pltpu
from jax.sharding import PartitionSpec as P

ITERS = 3
LANES = 128
MESH = pl.DeviceIdType.MESH


def pairwise(terms):
    while len(terms) > 1:
        terms = [
            terms[i] + terms[i + 1] if i + 1 < len(terms) else terms[i]
            for i in range(0, len(terms), 2)
        ]
    return terms[0]


def kernel(
    row_n, col_n, flows, mask, row_target, col_target, row_out, col_out,
    held, row_slots, col_slots, row_scale, col_scale, col_acc,
    load_sem, row_send, row_recv, col_send, col_recv,
):
    row_count, col_count = flows.shape
    row_tiles, col_tiles = row_count // LANES, col_count // LANES
    my_row, my_col = lax.axis_index("row"), lax.axis_index("col")

    loads = []
    for b in range(row_tiles):
        rows = pl.ds(b * LANES, LANES)
        load = pltpu.make_async_copy(flows.at[rows, :], held.at[rows, :], load_sem.at[b])
        load.start()
        loads.append(load)

    barrier = pltpu.get_barrier_semaphore()
    for d in range(1, col_n):
        pl.semaphore_signal(
            barrier, inc=1, device_id={"col": lax.rem(my_col + d, col_n)}, device_id_type=MESH
        )
    for d in range(1, row_n):
        pl.semaphore_signal(
            barrier, inc=1, device_id={"row": lax.rem(my_row + d, row_n)}, device_id_type=MESH
        )

    def block(b):
        return pl.ds(pl.multiple_of(b * LANES, LANES), LANES)

    def put_row_total(it, b, acc):
        row_slots[it, my_col, pl.ds(b, 1), :] = jnp.sum(acc.T, axis=0, keepdims=True)

    def exchange(slots, send, recv, it, axis, me, n):
        copies = []
        for d in range(1, n):
            copy = pltpu.make_async_remote_copy(
                src_ref=slots.at[it, me],
                dst_ref=slots.at[it, me],
                send_sem=send.at[it, d],
                recv_sem=recv.at[it, d],
                device_id={axis: lax.rem(me + d, n)},
                device_id_type=MESH,
            )
            copy.start()
            copies.append(copy)
        return copies

    for b in range(row_tiles):
        loads[b].wait()
        acc = jnp.zeros((LANES, LANES), jnp.float32)
        rows = slice(b * LANES, (b + 1) * LANES)
        for j in range(col_tiles):
            cols = slice(j * LANES, (j + 1) * LANES)
            value = held[rows, cols] * mask[b, j].astype(jnp.float32)
            held[rows, cols] = value
            acc = acc + value
        put_row_total(0, b, acc)

    pl.semaphore_wait(barrier, row_n + col_n - 2)

    unroll = 4 if row_tiles % 4 == 0 else 1
    sent = []
    for it in range(ITERS):
        if it > 0:
            def row_pass(step, carry):
                for u in range(unroll):
                    b = step * unroll + u
                    acc = None
                    for j in range(col_tiles):
                        cols = slice(j * LANES, (j + 1) * LANES)
                        term = held[block(b), cols] * col_scale[j : j + 1, :]
                        acc = term if acc is None else acc + term
                    put_row_total(it, b, acc)
                return carry

            lax.fori_loop(0, row_tiles // unroll, row_pass, 0)
        copies = exchange(row_slots, row_send, row_recv, it, "col", my_col, col_n)
        for copy in copies:
            copy.wait_recv()
        sent += copies
        total = pairwise([row_slots[it, k] for k in range(col_n)])
        row_scale[...] = (row_target[...].astype(jnp.float32) * 0.001) / total

        col_acc[...] = jnp.zeros_like(col_acc)

        def col_pass(step, carry):
            for u in range(unroll):
                b = step * unroll + u
                scale = jnp.broadcast_to(row_scale[pl.ds(b, 1), :], (LANES, LANES)).T
                for j in range(col_tiles):
                    cols = slice(j * LANES, (j + 1) * LANES)
                    term = held[block(b), cols] * scale
                    col_acc[j] += pairwise([term[g * 8 : g * 8 + 8] for g in range(LANES // 8)])
            return carry

        lax.fori_loop(0, row_tiles // unroll, col_pass, 0)
        col_slots[it, my_row] = jnp.sum(col_acc[...], axis=1)
        copies = exchange(col_slots, col_send, col_recv, it, "row", my_row, row_n)
        for b in range(row_tiles):
            row_out[it : it + 1, b * LANES : (b + 1) * LANES] = row_scale[b : b + 1, :]
        for copy in copies:
            copy.wait_recv()
        sent += copies
        total = pairwise([col_slots[it, k] for k in range(row_n)])
        col_scale[...] = (col_target[...].astype(jnp.float32) * 0.001) / total
        for j in range(col_tiles):
            col_out[it : it + 1, j * LANES : (j + 1) * LANES] = col_scale[j : j + 1, :]

    for copy in sent:
        copy.wait_send()


def shards(row_n, col_n, flows, tile_mask, row_target, col_target):
    row_count, col_count = flows.shape
    row_tiles, col_tiles = row_count // LANES, col_count // LANES
    vmem = pl.BlockSpec(memory_space=pltpu.VMEM)
    return pl.pallas_call(
        functools.partial(kernel, row_n, col_n),
        out_shape=(
            jax.ShapeDtypeStruct((ITERS, row_count), jnp.float32),
            jax.ShapeDtypeStruct((ITERS, col_count), jnp.float32),
        ),
        in_specs=[
            pl.BlockSpec(memory_space=pl.ANY),
            pl.BlockSpec(memory_space=pltpu.SMEM),
            vmem,
            vmem,
        ],
        out_specs=(vmem, vmem),
        scratch_shapes=[
            pltpu.VMEM((row_count, col_count), jnp.float32),
            pltpu.VMEM((ITERS, col_n, row_tiles, LANES), jnp.float32),
            pltpu.VMEM((ITERS, row_n, col_tiles, LANES), jnp.float32),
            pltpu.VMEM((row_tiles, LANES), jnp.float32),
            pltpu.VMEM((col_tiles, LANES), jnp.float32),
            pltpu.VMEM((col_tiles, 8, LANES), jnp.float32),
            pltpu.SemaphoreType.DMA((row_tiles,)),
            pltpu.SemaphoreType.DMA((ITERS, col_n)),
            pltpu.SemaphoreType.DMA((ITERS, col_n)),
            pltpu.SemaphoreType.DMA((ITERS, row_n)),
            pltpu.SemaphoreType.DMA((ITERS, row_n)),
        ],
        compiler_params=pltpu.CompilerParams(
            collective_id=0, has_side_effects=True, vmem_limit_bytes=60 * 1024 * 1024
        ),
    )(
        flows,
        tile_mask,
        row_target.reshape(row_tiles, LANES),
        col_target.reshape(col_tiles, LANES),
    )


def solution(mesh):
    return jax.shard_map(
        functools.partial(shards, mesh.shape["row"], mesh.shape["col"]),
        mesh=mesh,
        in_specs=(
            P(("batch", "row"), "col"),
            P(("batch", "row"), "col"),
            P(("batch", "row")),
            P(("batch", "col")),
        ),
        out_specs=(P("batch", "row"), P("batch", "col")),
        check_vma=False,
    )
```

time: 187 us -> 49.4 us (0.26)
  other arithmetic: 118 us -> 0 us
  blocking collectives: 46.5 us -> 0 us
  Pallas kernels: 0 us -> 45.6 us
  local copies, waits for them, and re-layouts: 20.1 us -> 2.86 us
    reduce_sum x6 -> x0, other arithmetic: 75.1 us -> none  [the longest x3 38.4 us: advance(): col_part = jnp.sum(active * row_scale[:, None], axis=0)]
    psum x6 -> x0, blocking collectives: 46.5 us -> none  [the longest x3 30.5 us: advance(): col_total = lax.psum(col_part, 'row')]
    pallas_call x0 -> x1, Pallas kernels: none -> 45.6 us  [shards(): pl.pallas_call(functools.partial(kernel, row_n, col_n), out_shape=(jax.Sh...]
    mul x3 -> x0, other arithmetic: 42.4 us -> none  [the longest x1 42.4 us: shards(): flows.reshape(row_count // tile_side, tile_side, col_count // tile_side,...]
    mul x1 -> x0, local copies, waits for them, and re-layouts: 11.2 us -> none  [shards(): flows.reshape(row_count // tile_side, tile_side, col_count // tile_side,...]
    dynamic_update_slice x6 -> x0, local copies, waits for them, and re-layouts: 8.88 us -> none  [the longest x3 4.64 us: advance(): lax.dynamic_update_slice_in_dim(col_hist, col_scale[None, :], sweep_index...]
    unnamed x4 -> x2, local copies, waits for them, and re-layouts: 0.01 us -> 2.86 us
where the time goes in v1:
time: 49.4 us; the launch traced here: 49.1 us
  Pallas kernels  45.6 us (92%)
  local copies, waits for them, and re-layouts  2.86 us (6%)
  between operations  0.64 us (1%)
    pallas_call x1, Pallas kernels, shards(): pl.pallas_call(functools.partial(kernel, row_n, col_n), out_shape=(jax.Sh...  45.6 us
    unnamed x2, local copies, waits for them, and re-layouts  2.86 us

profile of v1, /device:TPU:0, one launch (start us, length us, event | category | flops | bytes accessed | tf_op | source)
XLA Modules:
  0.0 49.1 jit_solution(10981692549188398933)
XLA Ops:
  0.6 45.6 %shard_map.59 = (f32[3,2048]{1,0:T(4,128)}, f32[3,4096]{1,0:T(4,128)}) custom-call(f32[2048,4096]{1,0:T(8,128)} %flows.1, s32[16,32]{1,0:T(8,128)} %mask.1, s32[16,128]{1,0:T(8,128)} %bitcast.3, s32[32,128]{1,0:T(8,128)} %bitcast.2), custom_call_target="tpu_custom_call" | custom-call | tf_op jit(solution)/shard_map/pallas_call | solution.py:140
  46.2 1.4 %copy.8 = f32[3,2048]{1,0:T(4,128)} copy(f32[3,2048]{1,0:T(4,128)} %get-tuple-element.4) | data formatting | bytes 49152
  47.6 1.5 %copy.9 = f32[3,4096]{1,0:T(4,128)} copy(f32[3,4096]{1,0:T(4,128)} %get-tuple-element.5) | data formatting | bytes 98304

commit v2 on v0

v2 whole, which is shorter than its diff:
```python
import functools

import jax
import jax.numpy as jnp
from jax import lax
from jax.experimental import pallas as pl
from jax.experimental.pallas import tpu as pltpu
from jax.sharding import PartitionSpec as P

ITERS = 3
LANES = 128
LAG = 3
MESH = pl.DeviceIdType.MESH


def pairwise(terms):
    while len(terms) > 1:
        terms = [
            terms[i] + terms[i + 1] if i + 1 < len(terms) else terms[i]
            for i in range(0, len(terms), 2)
        ]
    return terms[0]


def pieces_of(tiles, first):
    return [(0, first), (first, tiles)] if 0 < first < tiles else [(0, tiles)]


def kernel(
    row_n, col_n, flows, mask_in, row_target_in, col_target_in, row_hist, col_hist,
    held, first_slots, row_slots, col_slots, row_acc, col_acc, row_target, col_target, mask,
    load_sem, small_sem, first_send, first_recv, row_send, row_recv, col_send, col_recv,
):
    row_count, col_count = flows.shape
    row_tiles, col_tiles = row_count // LANES, col_count // LANES
    my_row, my_col = lax.axis_index("row"), lax.axis_index("col")
    chunks = first_slots.shape[1]
    per = row_tiles // chunks
    row_pieces = pieces_of(row_tiles, row_tiles // 16 * 8)
    col_pieces = pieces_of(col_tiles, col_tiles // 32 * 8)

    smalls = [
        pltpu.make_async_copy(source, target, small_sem.at[i])
        for i, (source, target) in enumerate(
            [(mask_in, mask), (row_target_in, row_target), (col_target_in, col_target)]
        )
    ]
    smalls[0].start()

    def load(k):
        rows = pl.ds(pl.multiple_of(k * per * LANES, LANES), per * LANES)
        return pltpu.make_async_copy(flows.at[rows, :], held.at[rows, :], load_sem.at[k])

    for k in range(chunks):
        load(k).start()
        if k == 0:
            smalls[1].start()
            smalls[2].start()

    barrier = pltpu.get_barrier_semaphore()
    for d in range(1, col_n):
        pl.semaphore_signal(
            barrier, inc=1, device_id={"col": lax.rem(my_col + d, col_n)}, device_id_type=MESH
        )
    for d in range(1, row_n):
        pl.semaphore_signal(
            barrier, inc=1, device_id={"row": lax.rem(my_row + d, row_n)}, device_id_type=MESH
        )
    first_slots[my_col] = jnp.zeros(first_slots.shape[1:], jnp.float32)
    col_acc[...] = jnp.zeros_like(col_acc)
    for small in smalls:
        small.wait()
    pl.semaphore_wait(barrier, row_n + col_n - 2)

    def block(b):
        return pl.ds(pl.multiple_of(b * LANES, LANES), LANES)

    def lanes(j):
        return slice(j * LANES, (j + 1) * LANES)

    def remote(ref, send, recv, axis, me, n, d):
        return pltpu.make_async_remote_copy(
            src_ref=ref,
            dst_ref=ref,
            send_sem=send.at[d],
            recv_sem=recv.at[d],
            device_id={axis: lax.rem(me + d, n)},
            device_id_type=MESH,
        )

    def first_copies(k):
        return [
            remote(
                first_slots.at[my_col, k], first_send.at[k], first_recv.at[k],
                "col", my_col, col_n, d,
            )
            for d in range(1, col_n)
        ]

    def row_copies(it, p):
        lo, hi = row_pieces[p]
        return [
            remote(
                row_slots.at[it, my_col, pl.ds(lo, hi - lo)], row_send.at[it, p],
                row_recv.at[it, p], "col", my_col, col_n, d,
            )
            for d in range(1, col_n)
        ]

    def col_copies(it, p):
        lo, hi = col_pieces[p]
        return [
            remote(
                col_slots.at[it, my_row, pl.ds(lo, hi - lo)], col_send.at[it, p],
                col_recv.at[it, p], "row", my_row, row_n, d,
            )
            for d in range(1, row_n)
        ]

    def start(copies):
        for copy in copies:
            copy.start()

    def arrive(copies):
        for copy in copies:
            copy.wait_recv()

    def add_cols(it, b, lo, hi):
        scale = jnp.broadcast_to(row_hist[it, pl.ds(b, 1), :], (LANES, LANES)).T
        for j in range(lo, hi):
            term = held[block(b), lanes(j)] * scale
            col_acc[j] += pairwise([term[g * 8 : g * 8 + 8] for g in range(LANES // 8)])

    def loop(lo, hi, body):
        count = hi - lo
        unroll = 4 if count % 4 == 0 else (2 if count % 2 == 0 else 1)

        def steps(step, carry):
            for u in range(unroll):
                body(lo + step * unroll + u)
            return carry

        lax.fori_loop(0, count // unroll, steps, 0)

    def send_cols(it, p):
        lo, hi = col_pieces[p]
        col_slots[it, my_row, lo:hi] = jnp.sum(col_acc[lo:hi], axis=1)
        start(col_copies(it, p))
        col_acc[lo:hi] = jnp.zeros((hi - lo, 8, LANES), jnp.float32)

    def take_cols(it, p):
        arrive(col_copies(it, p))
        lo, hi = col_pieces[p]
        total = pairwise([col_slots[it, m, lo:hi] for m in range(row_n)])
        col_hist[it, lo:hi] = (col_target[lo:hi].astype(jnp.float32) * 0.001) / total

    def first_rows(k):
        load(k).wait()
        for u in range(per):
            b = k * per + u
            acc = None
            for j in range(col_tiles):
                value = held[block(b), lanes(j)] * mask[b, j].astype(jnp.float32)
                held[block(b), lanes(j)] = value
                acc = value if acc is None else acc + value
            first_slots[my_col, k, u : u + 1, :] = jnp.sum(acc.T, axis=0, keepdims=True)
        start(first_copies(k))

    def first_take(k):
        arrive(first_copies(k))
        for u in range(per):
            b = k * per + u
            total = pairwise([first_slots[m, k, u : u + 1, :] for m in range(col_n)])
            goal = row_target[pl.ds(b, 1), :].astype(jnp.float32) * 0.001
            row_hist[0, pl.ds(b, 1), :] = goal / total

    def first_cols(k):
        first_take(k)
        for u in range(per):
            add_cols(0, k * per + u, 0, col_tiles)

    def prologue(k, carry):
        first_rows(k)
        return carry

    def steady(k, carry):
        first_rows(k)
        first_cols(k - LAG)
        return carry

    def epilogue(k, carry):
        first_cols(k)
        return carry

    lax.fori_loop(0, LAG, prologue, 0)
    lax.fori_loop(LAG, chunks, steady, 0)
    lax.fori_loop(chunks - LAG, chunks - 1, epilogue, 0)
    first_take(chunks - 1)
    for p, (lo, hi) in enumerate(col_pieces):
        for u in range(per):
            add_cols(0, (chunks - 1) * per + u, lo, hi)
        send_cols(0, p)

    def row_block(it, b, lo, hi, fresh):
        acc = None if fresh else row_acc[block(b), :]
        for j in range(lo, hi):
            term = held[block(b), lanes(j)] * col_hist[it - 1, j : j + 1, :]
            acc = term if acc is None else acc + term
        return acc

    for it in range(1, ITERS):
        for p, (lo, hi) in enumerate(col_pieces[:-1]):
            take_cols(it - 1, p)

            def partial(b):
                row_acc[block(b), :] = row_block(it, b, lo, hi, p == 0)

            loop(0, row_tiles, partial)
        last = len(col_pieces) - 1
        take_cols(it - 1, last)
        lo, hi = col_pieces[last]
        for p, (top, end) in enumerate(row_pieces):

            def whole(b):
                acc = row_block(it, b, lo, hi, last == 0)
                row_slots[it, my_col, pl.ds(b, 1), :] = jnp.sum(acc.T, axis=0, keepdims=True)

            loop(top, end, whole)
            start(row_copies(it, p))
        for p, (top, end) in enumerate(row_pieces):
            arrive(row_copies(it, p))
            total = pairwise([row_slots[it, m, top:end] for m in range(col_n)])
            row_hist[it, top:end] = (row_target[top:end].astype(jnp.float32) * 0.001) / total
            if p < len(row_pieces) - 1:
                loop(top, end, lambda b: add_cols(it, b, 0, col_tiles))
            else:
                for q, (lo, hi) in enumerate(col_pieces):
                    loop(top, end, lambda b: add_cols(it, b, lo, hi))
                    send_cols(it, q)

    for p in range(len(col_pieces)):
        take_cols(ITERS - 1, p)

    def drain(k, carry):
        for copy in first_copies(k):
            copy.wait_send()
        return carry

    lax.fori_loop(0, chunks, drain, 0)
    for it in range(ITERS):
        copies = [copy for p in range(len(col_pieces)) for copy in col_copies(it, p)]
        if it > 0:
            copies += [copy for p in range(len(row_pieces)) for copy in row_copies(it, p)]
        for copy in copies:
            copy.wait_send()


def close(row_hist, col_hist, row_out, col_out):
    for source, target in ((row_hist, row_out), (col_hist, col_out)):
        for j in range(source.shape[1]):
            target[:, j * LANES : (j + 1) * LANES] = source[:, j, :]


def shards(row_n, col_n, flows, tile_mask, row_target, col_target):
    row_count, col_count = flows.shape
    row_tiles, col_tiles = row_count // LANES, col_count // LANES
    chunks = row_tiles // 2 if row_tiles % 2 == 0 else row_tiles
    vmem = pl.BlockSpec(memory_space=pltpu.VMEM)
    dma = pltpu.SemaphoreType.DMA
    row_hist, col_hist = pl.pallas_call(
        functools.partial(kernel, row_n, col_n),
        out_shape=(
            pltpu.VMEM((ITERS, row_tiles, LANES), jnp.float32),
            pltpu.VMEM((ITERS, col_tiles, LANES), jnp.float32),
        ),
        in_specs=[pl.BlockSpec(memory_space=pl.ANY)] * 4,
        out_specs=(vmem, vmem),
        scratch_shapes=[
            pltpu.VMEM((row_count, col_count), jnp.float32),
            pltpu.VMEM((col_n, chunks, 8, LANES), jnp.float32),
            pltpu.VMEM((ITERS, col_n, row_tiles, LANES), jnp.float32),
            pltpu.VMEM((ITERS, row_n, col_tiles, LANES), jnp.float32),
            pltpu.VMEM((row_count, LANES), jnp.float32),
            pltpu.VMEM((col_tiles, 8, LANES), jnp.float32),
            pltpu.VMEM((row_tiles, LANES), jnp.int32),
            pltpu.VMEM((col_tiles, LANES), jnp.int32),
            pltpu.SMEM((row_tiles, col_tiles), jnp.int32),
            dma((chunks,)),
            dma((3,)),
            dma((chunks, col_n)),
            dma((chunks, col_n)),
            dma((ITERS, 2, col_n)),
            dma((ITERS, 2, col_n)),
            dma((ITERS, 2, row_n)),
            dma((ITERS, 2, row_n)),
        ],
        compiler_params=pltpu.CompilerParams(
            collective_id=0, has_side_effects=True, vmem_limit_bytes=56 * 1024 * 1024
        ),
    )(
        flows,
        tile_mask,
        row_target.reshape(row_tiles, LANES),
        col_target.reshape(col_tiles, LANES),
    )
    return pl.pallas_call(
        close,
        out_shape=(
            jax.ShapeDtypeStruct((ITERS, row_count), jnp.float32),
            jax.ShapeDtypeStruct((ITERS, col_count), jnp.float32),
        ),
        in_specs=[vmem, vmem],
        out_specs=(vmem, vmem),
    )(*(pltpu.with_memory_space_constraint(h, pltpu.VMEM) for h in (row_hist, col_hist)))


def solution(mesh):
    return jax.shard_map(
        functools.partial(shards, mesh.shape["row"], mesh.shape["col"]),
        mesh=mesh,
        in_specs=(
            P(("batch", "row"), "col"),
            P(("batch", "row"), "col"),
            P(("batch", "row")),
            P(("batch", "col")),
        ),
        out_specs=(P("batch", "row"), P("batch", "col")),
        check_vma=False,
    )
```

time: 187 us -> 46.2 us (0.25)
  other arithmetic: 118 us -> 0 us
  blocking collectives: 46.5 us -> 0 us
  Pallas kernels: 0 us -> 45.4 us
  local copies, waits for them, and re-layouts: 20.1 us -> 0 us
    reduce_sum x6 -> x0, other arithmetic: 75.1 us -> none  [the longest x3 38.4 us: advance(): col_part = jnp.sum(active * row_scale[:, None], axis=0)]
    psum x6 -> x0, blocking collectives: 46.5 us -> none  [the longest x3 30.5 us: advance(): col_total = lax.psum(col_part, 'row')]
    pallas_call x0 -> x2, Pallas kernels: none -> 45.4 us  [the longest x1 44.8 us: shards(): pl.pallas_call(functools.partial(kernel, row_n, col_n), out_shape=(pltpu....]
    mul x3 -> x0, other arithmetic: 42.4 us -> none  [the longest x1 42.4 us: shards(): flows.reshape(row_count // tile_side, tile_side, col_count // tile_side,...]
    mul x1 -> x0, local copies, waits for them, and re-layouts: 11.2 us -> none  [shards(): flows.reshape(row_count // tile_side, tile_side, col_count // tile_side,...]
    dynamic_update_slice x6 -> x0, local copies, waits for them, and re-layouts: 8.88 us -> none  [the longest x3 4.64 us: advance(): lax.dynamic_update_slice_in_dim(col_hist, col_scale[None, :], sweep_index...]
where the time goes in v2:
time: 46.2 us; the launch traced here: 46.1 us
  Pallas kernels  45.4 us (98%)
  between operations  0.64 us (1%)
    pallas_call x1, Pallas kernels, shards(): pl.pallas_call(functools.partial(kernel, row_n, col_n), out_shape=(pltpu....  44.8 us

profile of v2, /device:TPU:0, one launch (start us, length us, event | category | flops | bytes accessed | tf_op | source)
XLA Modules:
  0.0 46.1 jit_solution(3037987896991571295)
XLA Ops:
  0.6 44.8 %shard_map.59 = (f32[3,16,128]{2,1,0:T(8,128)S(1)}, f32[3,32,128]{2,1,0:T(8,128)S(1)}) custom-call(f32[2048,4096]{1,0:T(8,128)} %flows.1, s32[16,32]{1,0:T(8,128)} %mask_in.1, s32[16,128]{1,0:T(8,128)} %bitcast.3, s32[32,128]{1,0:T(8,128)} %bitcast.2), custom_call_target="tpu_custom_call" | custom-call | tf_op jit(solution)/shard_map/pallas_call | solution.py:270
  45.4 0.7 %shard_map.60 = (f32[3,2048]{1,0:T(4,128)}, f32[3,4096]{1,0:T(4,128)}) custom-call(f32[3,16,128]{2,1,0:T(8,128)S(1)} %get-tuple-element.4.row_hist, f32[3,32,128]{2,1,0:T(8,128)S(1)} %get-tuple-element.5.col_hist), custom_call_target="tpu_custom_call" | custom-call | tf_op jit(solution)/shard_map/pallas_call | solution.py:306
